TPU v7x, 32 devices: a whole 2x2x4 slice. The times are simulated.
32 devices in a mesh: row: 4 (over z), col: 8 (over y, x, core).
Axes of the slice: x: 2, y: 2, z: 4, core: 2. Of those that a mesh axis runs over, the one named last changes fastest.
Arguments:
- points: float32 [16, 32768], P(None, ('row', 'col')), may hold values from -6 to 6
- inverse_scales: float32 [16], replicated, may hold values from 0.05 to 31.255105
- probe_signs: int32 [32768, 128], P(('row', 'col')), may hold values 0 or 1
Outputs:
- trace_terms: float32 [128], replicated
- logdet_terms: float32 [128], replicated
All inputs are finite; a program needn't handle non-finite values. No bound on the sum of `probe_signs` on one device may be relied on, other than what follows from the above.
Results may differ from a plain program's by a relative error of at most 0.0014.
Values may be sent and summed in bfloat16 or wider, within the bound.
A program may use at most 128 MiB of HBM per device.

v0:
```python
import math
import jax
import jax.numpy as jnp
from jax import lax
from jax.sharding import PartitionSpec as P

STEPS = 3
epsilon = 1e-06
noise_level = 1.0
jacobi_sweeps = 6


def kernel_block(left_points, right_points):
    cross_term = lax.dot_general(
        left_points,
        right_points,
        (((0,), (0,)), ((), ())),
        precision=lax.Precision.HIGHEST,
        preferred_element_type=jnp.float32,
    )
    left_norms = jnp.sum(left_points * left_points, axis=0)
    right_norms = jnp.sum(right_points * right_points, axis=0)
    distance = jnp.maximum(left_norms[:, None] + right_norms[None, :] - 2.0 * cross_term, 0.0)
    return jnp.exp(-0.5 * distance).astype(jnp.bfloat16)


def form_blocks(row_points, col_points):
    total_rows = row_points.shape[1]
    block_rows = math.gcd(total_rows, 512)
    blocked = row_points.reshape(
        row_points.shape[0], total_rows // block_rows, block_rows
    ).transpose(1, 0, 2)
    stacked = lax.map(lambda block_points: kernel_block(block_points, col_points), blocked)
    return stacked.reshape(total_rows, col_points.shape[1])


def log_weight(alpha_list, beta_list):
    degree = len(alpha_list)
    width_probes = alpha_list[0].shape[0]
    zeros_row = jnp.zeros((width_probes,), jnp.float32)
    ones_row = jnp.ones((width_probes,), jnp.float32)
    matrix = []
    vectors = []
    for first_idx in range(degree):
        entries = []
        basis_row = []
        for second_idx in range(degree):
            if first_idx == second_idx:
                entries.append(alpha_list[first_idx])
                basis_row.append(ones_row)
            elif abs(first_idx - second_idx) == 1:
                entries.append(beta_list[min(first_idx, second_idx)])
                basis_row.append(zeros_row)
            else:
                entries.append(zeros_row)
                basis_row.append(zeros_row)
        matrix.append(entries)
        vectors.append(basis_row)
    for sweep_index in range(jacobi_sweeps):
        for first_idx in range(degree):
            for second_idx in range(first_idx + 1, degree):
                coupling = matrix[first_idx][second_idx]
                rotate_by = 0.5 * jnp.arctan2(
                    2.0 * coupling, matrix[second_idx][second_idx] - matrix[first_idx][first_idx]
                )
                cosine = jnp.cos(rotate_by)
                sine_val = jnp.sin(rotate_by)
                for row_idx in range(degree):
                    left_val = matrix[row_idx][first_idx]
                    right_val = matrix[row_idx][second_idx]
                    matrix[row_idx][first_idx] = cosine * left_val - sine_val * right_val
                    matrix[row_idx][second_idx] = sine_val * left_val + cosine * right_val
                    left_vec = vectors[row_idx][first_idx]
                    right_vec = vectors[row_idx][second_idx]
                    vectors[row_idx][first_idx] = cosine * left_vec - sine_val * right_vec
                    vectors[row_idx][second_idx] = sine_val * left_vec + cosine * right_vec
                for col_idx in range(degree):
                    upper_val = matrix[first_idx][col_idx]
                    lower_val = matrix[second_idx][col_idx]
                    matrix[first_idx][col_idx] = cosine * upper_val - sine_val * lower_val
                    matrix[second_idx][col_idx] = sine_val * upper_val + cosine * lower_val
    total = zeros_row
    for index_k in range(degree):
        total = total + vectors[0][index_k] * vectors[0][index_k] * jnp.log(
            matrix[index_k][index_k]
        )
    return total


def per_device(points, inverse_scales, probe_signs):
    scaled = points * inverse_scales[:, None]
    row_points = lax.all_gather(scaled, "col", axis=1, tiled=True)
    col_points = lax.all_gather(scaled, "row", axis=1, tiled=True)
    cached = form_blocks(row_points, col_points)
    direction = 2.0 * probe_signs.astype(jnp.float32) - 1.0
    basis_prev = jnp.zeros_like(direction)
    alpha_list = []
    beta_list = []
    for lanczos_step in range(STEPS):
        squares = lax.psum(jnp.sum(direction * direction, axis=0), ("row", "col"))
        vector_half = direction.astype(jnp.bfloat16)
        gathered = lax.all_gather(vector_half, "col", axis=0, tiled=True)
        image = (
            lax.psum_scatter(
                lax.dot_general(
                    cached, gathered, (((0,), (0,)), ((), ())), preferred_element_type=jnp.float32
                ).astype(jnp.bfloat16),
                "row",
                scatter_dimension=0,
                tiled=True,
            ).astype(jnp.float32)
            + noise_level * direction
        )
        curvature = lax.psum(jnp.sum(direction * image, axis=0), ("row", "col"))
        beta_now = jnp.sqrt(squares + epsilon)
        alpha_now = curvature / (beta_now * beta_now)
        alpha_list.append(alpha_now)
        beta_list.append(beta_now)
        if lanczos_step + 1 < STEPS:
            basis_now = direction / beta_now
            direction = image / beta_now - alpha_now * basis_now - beta_now * basis_prev
            basis_prev = basis_now
    logdet_terms = log_weight(alpha_list, beta_list[1:])
    return (alpha_list[0], logdet_terms)


def solution(mesh):
    in_specs = (P(None, ("row", "col")), P(), P(("row", "col"), None))
    out_specs = (P(), P())
    return jax.shard_map(
        per_device, mesh=mesh, in_specs=in_specs, out_specs=out_specs, check_vma=False
    )
```

profile of v0, /device:TPU:0, one launch (start us, length us, event | category | flops | bytes accessed | tf_op | source)
XLA Modules:
  0.0 559.0 jit_solution(14007900071963346204)
XLA Ops:
  7.2 0.0 all-gather.4.cloned.1.call-start
  7.2 1.8 fusion.8
  9.0 0.0 all-gather.4.cloned.1.call-update
  9.1 0.0 reduce-scatter.4.cloned.1.call-start
  9.1 0.9 broadcast_multiply_fusion
  10.0 15.6 %all_gather.16 = f32[16,4096]{1,0:T(8,128)S(1)} all-gather(f32[16,1024]{1,0:T(8,128)S(1)} %broadcast_multiply_fusion), channel_id=1, replica_groups=mesh['row'=4,'col'=8] {'row'}, dimensions={1}, use_global_device_ids=true | all-gather | bytes 327680 | tf_op jit(solution)/shard_map/all_gather | solution.py:93
  25.7 11.0 %all_gather.15 = f32[16,8192]{1,0:T(8,128)S(1)} all-gather(f32[16,1024]{1,0:T(8,128)S(1)} %broadcast_multiply_fusion), channel_id=1, replica_groups=mesh['row'=4,'col'=8] {'col'}, dimensions={1}, use_global_device_ids=true | all-gather | bytes 589824 | tf_op jit(solution)/shard_map/all_gather | solution.py:92
  36.8 163.7 %while.12 = (s32[]{:T(128)}, bf16[16,512,4096]{2,1,0:T(8,128)(2,1)}, f32[16,16,512]{2,1,0:T(8,128)S(1)}, f32[4096]{0:T(1024)S(1)}, f32[16,4096]{1,0:T(8,128)S(1)}, /*index=5*/s32[]{:T(128)}) while((s32[]{:T(128)}, bf16[16,512,4096]{2,1,0:T(8,128)(2,1)}, f32[16,16,512]{2,1,0:T(8,128)S(1)}, f32[4096]{0:T(1024)S(1)}, f32[16,4096]{1,0:T(8,128)S(1)}, ...), condition=%wide.region_3.4_spmd, body=%wide.region_1.3_spmd.sunk | while | flops 415251968 | bytes 4543561 | solution.py:33
  36.8 10.2 %fusion.25 = bf16[16,512,4096]{2,1,0:T(8,128)(2,1)} fusion(bf16[16,512,4096]{2,1,0:T(8,128)(2,1)} %get-tuple-element.127, s32[]{:T(128)} %get-tuple-element.126, f32[16,4096]{1,0:T(8,128)S(1)} %get-tuple-element.136, f32[4096]{0:T(1024)S(1)} %get-tuple-element.135, f32[512]{0:T(512)S(1)} %fusion.24, f32[16,16,512]{2,1,0:T(8,128)S(1)} %get-tuple-element.134), kind=kOutput, calls=%fused_computation.2.clone.1 | convolution fusion | flops 415236096 | bytes 4508672 | tf_op jit(solution)/shard_map/while/body/eval_jaxpr/dot_general | solution.py:14
  47.1 10.2 %fusion.25 = bf16[16,512,4096]{2,1,0:T(8,128)(2,1)} fusion(bf16[16,512,4096]{2,1,0:T(8,128)(2,1)} %get-tuple-element.127, s32[]{:T(128)} %get-tuple-element.126, f32[16,4096]{1,0:T(8,128)S(1)} %get-tuple-element.136, f32[4096]{0:T(1024)S(1)} %get-tuple-element.135, f32[512]{0:T(512)S(1)} %fusion.24, f32[16,16,512]{2,1,0:T(8,128)S(1)} %get-tuple-element.134), kind=kOutput, calls=%fused_computation.2.clone.1 | convolution fusion | flops 415236096 | bytes 4508672 | tf_op jit(solution)/shard_map/while/body/eval_jaxpr/dot_general | solution.py:14
  57.3 10.2 %fusion.25 = bf16[16,512,4096]{2,1,0:T(8,128)(2,1)} fusion(bf16[16,512,4096]{2,1,0:T(8,128)(2,1)} %get-tuple-element.127, s32[]{:T(128)} %get-tuple-element.126, f32[16,4096]{1,0:T(8,128)S(1)} %get-tuple-element.136, f32[4096]{0:T(1024)S(1)} %get-tuple-element.135, f32[512]{0:T(512)S(1)} %fusion.24, f32[16,16,512]{2,1,0:T(8,128)S(1)} %get-tuple-element.134), kind=kOutput, calls=%fused_computation.2.clone.1 | convolution fusion | flops 415236096 | bytes 4508672 | tf_op jit(solution)/shard_map/while/body/eval_jaxpr/dot_general | solution.py:14
  67.5 10.2 %fusion.25 = bf16[16,512,4096]{2,1,0:T(8,128)(2,1)} fusion(bf16[16,512,4096]{2,1,0:T(8,128)(2,1)} %get-tuple-element.127, s32[]{:T(128)} %get-tuple-element.126, f32[16,4096]{1,0:T(8,128)S(1)} %get-tuple-element.136, f32[4096]{0:T(1024)S(1)} %get-tuple-element.135, f32[512]{0:T(512)S(1)} %fusion.24, f32[16,16,512]{2,1,0:T(8,128)S(1)} %get-tuple-element.134), kind=kOutput, calls=%fused_computation.2.clone.1 | convolution fusion | flops 415236096 | bytes 4508672 | tf_op jit(solution)/shard_map/while/body/eval_jaxpr/dot_general | solution.py:14
  77.8 10.2 %fusion.25 = bf16[16,512,4096]{2,1,0:T(8,128)(2,1)} fusion(bf16[16,512,4096]{2,1,0:T(8,128)(2,1)} %get-tuple-element.127, s32[]{:T(128)} %get-tuple-element.126, f32[16,4096]{1,0:T(8,128)S(1)} %get-tuple-element.136, f32[4096]{0:T(1024)S(1)} %get-tuple-element.135, f32[512]{0:T(512)S(1)} %fusion.24, f32[16,16,512]{2,1,0:T(8,128)S(1)} %get-tuple-element.134), kind=kOutput, calls=%fused_computation.2.clone.1 | convolution fusion | flops 415236096 | bytes 4508672 | tf_op jit(solution)/shard_map/while/body/eval_jaxpr/dot_general | solution.py:14
  88.0 10.2 %fusion.25 = bf16[16,512,4096]{2,1,0:T(8,128)(2,1)} fusion(bf16[16,512,4096]{2,1,0:T(8,128)(2,1)} %get-tuple-element.127, s32[]{:T(128)} %get-tuple-element.126, f32[16,4096]{1,0:T(8,128)S(1)} %get-tuple-element.136, f32[4096]{0:T(1024)S(1)} %get-tuple-element.135, f32[512]{0:T(512)S(1)} %fusion.24, f32[16,16,512]{2,1,0:T(8,128)S(1)} %get-tuple-element.134), kind=kOutput, calls=%fused_computation.2.clone.1 | convolution fusion | flops 415236096 | bytes 4508672 | tf_op jit(solution)/shard_map/while/body/eval_jaxpr/dot_general | solution.py:14
  98.2 10.2 %fusion.25 = bf16[16,512,4096]{2,1,0:T(8,128)(2,1)} fusion(bf16[16,512,4096]{2,1,0:T(8,128)(2,1)} %get-tuple-element.127, s32[]{:T(128)} %get-tuple-element.126, f32[16,4096]{1,0:T(8,128)S(1)} %get-tuple-element.136, f32[4096]{0:T(1024)S(1)} %get-tuple-element.135, f32[512]{0:T(512)S(1)} %fusion.24, f32[16,16,512]{2,1,0:T(8,128)S(1)} %get-tuple-element.134), kind=kOutput, calls=%fused_computation.2.clone.1 | convolution fusion | flops 415236096 | bytes 4508672 | tf_op jit(solution)/shard_map/while/body/eval_jaxpr/dot_general | solution.py:14
  108.4 10.2 %fusion.25 = bf16[16,512,4096]{2,1,0:T(8,128)(2,1)} fusion(bf16[16,512,4096]{2,1,0:T(8,128)(2,1)} %get-tuple-element.127, s32[]{:T(128)} %get-tuple-element.126, f32[16,4096]{1,0:T(8,128)S(1)} %get-tuple-element.136, f32[4096]{0:T(1024)S(1)} %get-tuple-element.135, f32[512]{0:T(512)S(1)} %fusion.24, f32[16,16,512]{2,1,0:T(8,128)S(1)} %get-tuple-element.134), kind=kOutput, calls=%fused_computation.2.clone.1 | convolution fusion | flops 415236096 | bytes 4508672 | tf_op jit(solution)/shard_map/while/body/eval_jaxpr/dot_general | solution.py:14
  118.6 10.3 %fusion.25 = bf16[16,512,4096]{2,1,0:T(8,128)(2,1)} fusion(bf16[16,512,4096]{2,1,0:T(8,128)(2,1)} %get-tuple-element.127, s32[]{:T(128)} %get-tuple-element.126, f32[16,4096]{1,0:T(8,128)S(1)} %get-tuple-element.136, f32[4096]{0:T(1024)S(1)} %get-tuple-element.135, f32[512]{0:T(512)S(1)} %fusion.24, f32[16,16,512]{2,1,0:T(8,128)S(1)} %get-tuple-element.134), kind=kOutput, calls=%fused_computation.2.clone.1 | convolution fusion | flops 415236096 | bytes 4508672 | tf_op jit(solution)/shard_map/while/body/eval_jaxpr/dot_general | solution.py:14
  128.9 10.2 %fusion.25 = bf16[16,512,4096]{2,1,0:T(8,128)(2,1)} fusion(bf16[16,512,4096]{2,1,0:T(8,128)(2,1)} %get-tuple-element.127, s32[]{:T(128)} %get-tuple-element.126, f32[16,4096]{1,0:T(8,128)S(1)} %get-tuple-element.136, f32[4096]{0:T(1024)S(1)} %get-tuple-element.135, f32[512]{0:T(512)S(1)} %fusion.24, f32[16,16,512]{2,1,0:T(8,128)S(1)} %get-tuple-element.134), kind=kOutput, calls=%fused_computation.2.clone.1 | convolution fusion | flops 415236096 | bytes 4508672 | tf_op jit(solution)/shard_map/while/body/eval_jaxpr/dot_general | solution.py:14
  139.2 10.2 %fusion.25 = bf16[16,512,4096]{2,1,0:T(8,128)(2,1)} fusion(bf16[16,512,4096]{2,1,0:T(8,128)(2,1)} %get-tuple-element.127, s32[]{:T(128)} %get-tuple-element.126, f32[16,4096]{1,0:T(8,128)S(1)} %get-tuple-element.136, f32[4096]{0:T(1024)S(1)} %get-tuple-element.135, f32[512]{0:T(512)S(1)} %fusion.24, f32[16,16,512]{2,1,0:T(8,128)S(1)} %get-tuple-element.134), kind=kOutput, calls=%fused_computation.2.clone.1 | convolution fusion | flops 415236096 | bytes 4508672 | tf_op jit(solution)/shard_map/while/body/eval_jaxpr/dot_general | solution.py:14
  149.4 10.2 %fusion.25 = bf16[16,512,4096]{2,1,0:T(8,128)(2,1)} fusion(bf16[16,512,4096]{2,1,0:T(8,128)(2,1)} %get-tuple-element.127, s32[]{:T(128)} %get-tuple-element.126, f32[16,4096]{1,0:T(8,128)S(1)} %get-tuple-element.136, f32[4096]{0:T(1024)S(1)} %get-tuple-element.135, f32[512]{0:T(512)S(1)} %fusion.24, f32[16,16,512]{2,1,0:T(8,128)S(1)} %get-tuple-element.134), kind=kOutput, calls=%fused_computation.2.clone.1 | convolution fusion | flops 415236096 | bytes 4508672 | tf_op jit(solution)/shard_map/while/body/eval_jaxpr/dot_general | solution.py:14
  159.6 10.3 %fusion.25 = bf16[16,512,4096]{2,1,0:T(8,128)(2,1)} fusion(bf16[16,512,4096]{2,1,0:T(8,128)(2,1)} %get-tuple-element.127, s32[]{:T(128)} %get-tuple-element.126, f32[16,4096]{1,0:T(8,128)S(1)} %get-tuple-element.136, f32[4096]{0:T(1024)S(1)} %get-tuple-element.135, f32[512]{0:T(512)S(1)} %fusion.24, f32[16,16,512]{2,1,0:T(8,128)S(1)} %get-tuple-element.134), kind=kOutput, calls=%fused_computation.2.clone.1 | convolution fusion | flops 415236096 | bytes 4508672 | tf_op jit(solution)/shard_map/while/body/eval_jaxpr/dot_general | solution.py:14
  169.9 10.2 %fusion.25 = bf16[16,512,4096]{2,1,0:T(8,128)(2,1)} fusion(bf16[16,512,4096]{2,1,0:T(8,128)(2,1)} %get-tuple-element.127, s32[]{:T(128)} %get-tuple-element.126, f32[16,4096]{1,0:T(8,128)S(1)} %get-tuple-element.136, f32[4096]{0:T(1024)S(1)} %get-tuple-element.135, f32[512]{0:T(512)S(1)} %fusion.24, f32[16,16,512]{2,1,0:T(8,128)S(1)} %get-tuple-element.134), kind=kOutput, calls=%fused_computation.2.clone.1 | convolution fusion | flops 415236096 | bytes 4508672 | tf_op jit(solution)/shard_map/while/body/eval_jaxpr/dot_general | solution.py:14
  180.1 10.2 %fusion.25 = bf16[16,512,4096]{2,1,0:T(8,128)(2,1)} fusion(bf16[16,512,4096]{2,1,0:T(8,128)(2,1)} %get-tuple-element.127, s32[]{:T(128)} %get-tuple-element.126, f32[16,4096]{1,0:T(8,128)S(1)} %get-tuple-element.136, f32[4096]{0:T(1024)S(1)} %get-tuple-element.135, f32[512]{0:T(512)S(1)} %fusion.24, f32[16,16,512]{2,1,0:T(8,128)S(1)} %get-tuple-element.134), kind=kOutput, calls=%fused_computation.2.clone.1 | convolution fusion | flops 415236096 | bytes 4508672 | tf_op jit(solution)/shard_map/while/body/eval_jaxpr/dot_general | solution.py:14
  190.3 10.2 %fusion.25 = bf16[16,512,4096]{2,1,0:T(8,128)(2,1)} fusion(bf16[16,512,4096]{2,1,0:T(8,128)(2,1)} %get-tuple-element.127, s32[]{:T(128)} %get-tuple-element.126, f32[16,4096]{1,0:T(8,128)S(1)} %get-tuple-element.136, f32[4096]{0:T(1024)S(1)} %get-tuple-element.135, f32[512]{0:T(512)S(1)} %fusion.24, f32[16,16,512]{2,1,0:T(8,128)S(1)} %get-tuple-element.134), kind=kOutput, calls=%fused_computation.2.clone.1 | convolution fusion | flops 415236096 | bytes 4508672 | tf_op jit(solution)/shard_map/while/body/eval_jaxpr/dot_general | solution.py:14
  200.5 0.0 all-gather.4.cloned.1.call-done
  200.5 0.0 copy-start
  200.5 29.2 %convolution_convert_fusion.2 = bf16[4096,128]{1,0:T(8,128)(2,1)} fusion(bf16[8192,4096]{1,0:T(8,128)(2,1)} %bitcast.3, bf16[8192,128]{1,0:T(8,128)(2,1)} %all-gather.4.cloned.1.call-done), kind=kOutput, calls=%fused_computation.10 | convolution fusion | flops 8590458880 | bytes 70254592 | tf_op jit(solution)/shard_map/dot_general | solution.py:105
  229.7 0.0 reduce-scatter.4.cloned.1.call-update
  229.7 0.0 all-gather.6.cloned.1.call-start
  229.7 28.3 %reduce-scatter.4.cloned.1.call-done = bf16[1024,128]{1,0:T(8,128)(2,1)} async-done(((bf16[4096,128]{1,0:T(8,128)(2,1)}), bf16[1024,128]{1,0:T(8,128)(2,1)}) %reduce-scatter.4.cloned.1.call-update) | async-done | bytes 262160 | tf_op jit(solution)/shard_map/reduce_scatter | solution.py:104
  258.1 0.0 copy-done
  258.1 1.1 multiply_reduce_fusion.3
  259.2 38.9 %all-reduce.2 = (f32[128]{0:T(128)S(1)}, f32[128]{0:T(128)S(1)}) all-reduce(f32[128]{0:T(128)S(1)} %get-tuple-element.63, f32[128]{0:T(128)S(1)} %get-tuple-element.62), channel_id=1, replica_groups=mesh['row'=4,'col'=8] {'row','col'}, use_global_device_ids=true, to_apply=%region_6.7 | all-reduce | flops 256 | bytes 2048 | tf_op jit(solution)/shard_map/psum | solution.py:114
  298.1 0.0 copy-start.1
  298.1 1.9 fusion.10
  299.9 0.0 all-gather.6.cloned.1.call-update
  300.0 0.0 reduce-scatter.6.cloned.1.call-start
  300.0 27.6 %all-gather.6.cloned.1.call-done = bf16[8192,128]{1,0:T(8,128)(2,1)} async-done(((bf16[1024,128]{1,0:T(8,128)(2,1)}), bf16[8192,128]{1,0:T(8,128)(2,1)}) %all-gather.6.cloned.1.call-update) | async-done | bytes 2097168 | tf_op jit(solution)/shard_map/all_gather | solution.py:102
  327.6 29.1 %convolution_convert_fusion.1 = bf16[4096,128]{1,0:T(8,128)(2,1)} fusion(bf16[8192,4096]{1,0:T(8,128)(2,1)} %bitcast.3, bf16[8192,128]{1,0:T(8,128)(2,1)} %all-gather.6.cloned.1.call-done), kind=kOutput, calls=%fused_computation.9 | convolution fusion | flops 8590458880 | bytes 70254592 | tf_op jit(solution)/shard_map/dot_general | solution.py:105
  356.8 0.0 reduce-scatter.6.cloned.1.call-update
  356.8 0.0 all-gather.8.cloned.1.call-start
  356.8 27.4 %reduce-scatter.6.cloned.1.call-done = bf16[1024,128]{1,0:T(8,128)(2,1)} async-done(((bf16[4096,128]{1,0:T(8,128)(2,1)}), bf16[1024,128]{1,0:T(8,128)(2,1)}) %reduce-scatter.6.cloned.1.call-update) | async-done | bytes 262160 | tf_op jit(solution)/shard_map/reduce_scatter | solution.py:104
  384.2 1.1 multiply_reduce_fusion.2
  385.3 38.7 %all-reduce.1 = (f32[128]{0:T(128)S(1)}, f32[128]{0:T(128)S(1)}) all-reduce(f32[128]{0:T(128)S(1)} %get-tuple-element.61, f32[128]{0:T(128)S(1)} %get-tuple-element.60), channel_id=1, replica_groups=mesh['row'=4,'col'=8] {'row','col'}, use_global_device_ids=true, to_apply=%region_13.14 | all-reduce | flops 256 | bytes 2048 | tf_op jit(solution)/shard_map/psum | solution.py:114
  424.1 1.9 fusion.9
  426.0 0.0 all-gather.8.cloned.1.call-update
  426.0 0.3 reduce-scatter.8.cloned.1.call-start
  426.3 27.4 %all-gather.8.cloned.1.call-done = bf16[8192,128]{1,0:T(8,128)(2,1)} async-done(((bf16[1024,128]{1,0:T(8,128)(2,1)}), bf16[8192,128]{1,0:T(8,128)(2,1)}) %all-gather.8.cloned.1.call-update) | async-done | bytes 2097168 | tf_op jit(solution)/shard_map/all_gather | solution.py:102
  453.7 29.1 %convolution_convert_fusion = bf16[4096,128]{1,0:T(8,128)(2,1)} fusion(bf16[8192,4096]{1,0:T(8,128)(2,1)} %bitcast.3, bf16[8192,128]{1,0:T(8,128)(2,1)} %all-gather.8.cloned.1.call-done), kind=kOutput, calls=%fused_computation.8 | convolution fusion | flops 8590458880 | bytes 70254592 | tf_op jit(solution)/shard_map/dot_general | solution.py:105
  482.8 0.0 reduce-scatter.8.cloned.1.call-update
  482.8 27.4 %reduce-scatter.8.cloned.1.call-done = bf16[1024,128]{1,0:T(8,128)(2,1)} async-done(((bf16[4096,128]{1,0:T(8,128)(2,1)}), bf16[1024,128]{1,0:T(8,128)(2,1)}) %reduce-scatter.8.cloned.1.call-update) | async-done | bytes 262160 | tf_op jit(solution)/shard_map/reduce_scatter | solution.py:104
  510.3 1.1 multiply_reduce_fusion
  511.4 38.7 %all-reduce = (f32[128]{0:T(128)S(1)}, f32[128]{0:T(128)S(1)}) all-reduce(f32[128]{0:T(128)S(1)} %get-tuple-element.59, f32[128]{0:T(128)S(1)} %get-tuple-element.58), channel_id=1, replica_groups=mesh['row'=4,'col'=8] {'row','col'}, use_global_device_ids=true, to_apply=%region_18.19 | all-reduce | flops 256 | bytes 2048 | tf_op jit(solution)/shard_map/psum | solution.py:114
  550.1 0.0 copy-done.1
  550.1 2.0 multiply_add_fusion.1
  (21 shorter events, 0.5 us)
Async XLA Ops:
  7.2 193.3 %all-gather.4.cloned.1.call-start = ((), (), s32[]{:S(2)}) async-start(), calls=%async_computation.3 | async-start | bytes 2359296 | tf_op jit(solution)/shard_map/all_gather | solution.py:102
  9.1 249.0 %reduce-scatter.4.cloned.1.call-start = ((), (), s32[]{:S(2)}) async-start(), calls=%async_computation.4 | async-start | bytes 1310720 | tf_op jit(solution)/shard_map/reduce_scatter | solution.py:104
  200.5 57.5 %copy-start = (s32[1024,128]{1,0:T(8,128)S(1)}, s32[1024,128]{1,0:T(8,128)}, u32[]{:S(2)}) copy-start(s32[1024,128]{1,0:T(8,128)} %param.7) | copy-start | bytes 1572868
  229.7 98.0 %all-gather.6.cloned.1.call-start = ((), (), s32[]{:S(2)}) async-start(), calls=%async_computation.5 | async-start | bytes 2359296 | tf_op jit(solution)/shard_map/all_gather | solution.py:102
  298.1 252.0 %copy-start.1 = (f32[128]{0:T(128)}, f32[128]{0:T(128)S(1)}, u32[]{:S(2)}) copy-start(f32[128]{0:T(128)S(1)} %get-tuple-element.87) | copy-start | bytes 1540
  300.0 84.3 %reduce-scatter.6.cloned.1.call-start = ((), (), s32[]{:S(2)}) async-start(), calls=%async_computation.6 | async-start | bytes 1310720 | tf_op jit(solution)/shard_map/reduce_scatter | solution.py:104
  356.8 96.9 %all-gather.8.cloned.1.call-start = ((), (), s32[]{:S(2)}) async-start(), calls=%async_computation.7 | async-start | bytes 2359296 | tf_op jit(solution)/shard_map/all_gather | solution.py:102
  426.0 84.3 %reduce-scatter.8.cloned.1.call-start = ((), (), s32[]{:S(2)}) async-start(), calls=%async_computation.8 | async-start | bytes 1310720 | tf_op jit(solution)/shard_map/reduce_scatter | solution.py:104
Sparse Core Ops, SparseCore 0:
  9.9 31.1 all-gather.3
  229.8 28.1 reduce-scatter.3
  300.1 27.5 all-gather.5
  356.9 27.2 reduce-scatter.5
  426.1 27.5 all-gather.7
  482.9 27.2 reduce-scatter.7
where the time goes:
time: 560 us; the launch traced here: 559 us
  matrix products  251 us (45%)
  blocking collectives  143 us (26%)
  waiting for transfers between devices  138 us (25%)
  between operations  14.1 us (3%)
  other arithmetic  12.3 us (2%)
    dot_general x16, matrix products, kernel_block(): lax.dot_general(left_points, right_points, (((0,), (0,)), ((), ())), prec...  163 us
    psum x3, blocking collectives, per_device(): curvature = lax.psum(jnp.sum(direction * image, axis=0), ('row', 'col'))  116 us
    dot_general x3, matrix products, per_device(): lax.dot_general(cached, gathered, (((0,), (0,)), ((), ())), preferred_ele...  87.4 us
    reduce_scatter x3, waiting for transfers between devices, per_device(): lax.psum_scatter(lax.dot_general(cached, gathered, (((0,), (0,)), ((), ()...  83.2 us
    all_gather x3, waiting for transfers between devices, per_device(): gathered = lax.all_gather(vector_half, 'col', axis=0, tiled=True)  55.1 us
    all_gather x1, blocking collectives, per_device(): col_points = lax.all_gather(scaled, 'row', axis=1, tiled=True)  15.6 us
  transfers between devices with their start and end apart: 6, of which 5 were waited for; matrix products, arithmetic and copies ran while one was open for 29% of the time, Pallas kernels for 0%

commit v1 on v0

--- a/solution.py
+++ b/solution.py
@@ -111,7 +111,11 @@
             ).astype(jnp.float32)
             + noise_level * direction
         )
-        curvature = lax.psum(jnp.sum(direction * image, axis=0), ("row", "col"))
+
+        def state_connect(in_array):
+            return jax.lax.psum(jax.lax.psum(in_array, "col"), "row")
+
+        curvature = state_connect(jnp.sum(direction * image, axis=0))
         beta_now = jnp.sqrt(squares + epsilon)
         alpha_now = curvature / (beta_now * beta_now)
         alpha_list.append(alpha_now)

time: 560 us -> 626 us (1.12)
  blocking collectives: 143 us -> 210 us
    psum x3 -> x9, blocking collectives: 116 us -> 184 us  [the longest x3 116 us: per_device(): squares = lax.psum(jnp.sum(direction * direction, axis=0), ('row', 'col'))]
  transfers between devices with their start and end apart: 6 -> 6, of which waited for: 5 -> 5; matrix products, arithmetic and copies ran while one was open for 29% -> 26% of each run, Pallas kernels for 0% -> 0%
where the time goes in v1:
time: 626 us; the launch traced here: 625 us
  matrix products  251 us (40%)
  blocking collectives  210 us (34%)
  waiting for transfers between devices  137 us (22%)
  between operations  14.1 us (2%)
  other arithmetic  12.3 us (2%)
    dot_general x16, matrix products, kernel_block(): lax.dot_general(left_points, right_points, (((0,), (0,)), ((), ())), prec...  163 us
    psum x3, blocking collectives, per_device(): squares = lax.psum(jnp.sum(direction * direction, axis=0), ('row', 'col'))  116 us
    dot_general x3, matrix products, per_device(): lax.dot_general(cached, gathered, (((0,), (0,)), ((), ())), preferred_ele...  87.4 us
    reduce_scatter x3, waiting for transfers between devices, per_device(): lax.psum_scatter(lax.dot_general(cached, gathered, (((0,), (0,)), ((), ()...  83.2 us
    psum x6, blocking collectives, state_connect(): return jax.lax.psum(jax.lax.psum(in_array, 'col'), 'row')  67.2 us
    all_gather x3, waiting for transfers between devices, per_device(): gathered = lax.all_gather(vector_half, 'col', axis=0, tiled=True)  53.6 us
    all_gather x1, blocking collectives, per_device(): col_points = lax.all_gather(scaled, 'row', axis=1, tiled=True)  15.6 us
  transfers between devices with their start and end apart: 6, of which 5 were waited for; matrix products, arithmetic and copies ran while one was open for 26% of the time, Pallas kernels for 0%

profile of v1, /device:TPU:0, one launch (start us, length us, event | category | flops | bytes accessed | tf_op | source)
XLA Modules:
  0.0 624.9 jit_solution(13648169769022380451)
XLA Ops:
  7.2 0.0 all-gather.4.cloned.1.call-start
  7.2 1.8 fusion.8
  9.0 0.0 all-gather.4.cloned.1.call-update
  9.1 0.0 reduce-scatter.4.cloned.1.call-start
  9.1 0.9 broadcast_multiply_fusion
  10.0 15.6 %all_gather.16 = f32[16,4096]{1,0:T(8,128)S(1)} all-gather(f32[16,1024]{1,0:T(8,128)S(1)} %broadcast_multiply_fusion), channel_id=1, replica_groups=mesh['row'=4,'col'=8] {'row'}, dimensions={1}, use_global_device_ids=true | all-gather | bytes 327680 | tf_op jit(solution)/shard_map/all_gather | solution.py:93
  25.7 11.0 %all_gather.15 = f32[16,8192]{1,0:T(8,128)S(1)} all-gather(f32[16,1024]{1,0:T(8,128)S(1)} %broadcast_multiply_fusion), channel_id=1, replica_groups=mesh['row'=4,'col'=8] {'col'}, dimensions={1}, use_global_device_ids=true | all-gather | bytes 589824 | tf_op jit(solution)/shard_map/all_gather | solution.py:92
  36.8 163.7 %while.12 = (s32[]{:T(128)}, bf16[16,512,4096]{2,1,0:T(8,128)(2,1)}, f32[16,16,512]{2,1,0:T(8,128)S(1)}, f32[4096]{0:T(1024)S(1)}, f32[16,4096]{1,0:T(8,128)S(1)}, /*index=5*/s32[]{:T(128)}) while((s32[]{:T(128)}, bf16[16,512,4096]{2,1,0:T(8,128)(2,1)}, f32[16,16,512]{2,1,0:T(8,128)S(1)}, f32[4096]{0:T(1024)S(1)}, f32[16,4096]{1,0:T(8,128)S(1)}, ...), condition=%wide.region_3.4_spmd, body=%wide.region_1.3_spmd.sunk | while | flops 415251968 | bytes 4543561 | solution.py:33
  36.8 10.2 %fusion.25 = bf16[16,512,4096]{2,1,0:T(8,128)(2,1)} fusion(bf16[16,512,4096]{2,1,0:T(8,128)(2,1)} %get-tuple-element.121, s32[]{:T(128)} %get-tuple-element.120, f32[16,4096]{1,0:T(8,128)S(1)} %get-tuple-element.130, f32[4096]{0:T(1024)S(1)} %get-tuple-element.129, f32[512]{0:T(512)S(1)} %fusion.24, f32[16,16,512]{2,1,0:T(8,128)S(1)} %get-tuple-element.128), kind=kOutput, calls=%fused_computation.2.clone.1 | convolution fusion | flops 415236096 | bytes 4508672 | tf_op jit(solution)/shard_map/while/body/eval_jaxpr/dot_general | solution.py:14
  47.1 10.2 %fusion.25 = bf16[16,512,4096]{2,1,0:T(8,128)(2,1)} fusion(bf16[16,512,4096]{2,1,0:T(8,128)(2,1)} %get-tuple-element.121, s32[]{:T(128)} %get-tuple-element.120, f32[16,4096]{1,0:T(8,128)S(1)} %get-tuple-element.130, f32[4096]{0:T(1024)S(1)} %get-tuple-element.129, f32[512]{0:T(512)S(1)} %fusion.24, f32[16,16,512]{2,1,0:T(8,128)S(1)} %get-tuple-element.128), kind=kOutput, calls=%fused_computation.2.clone.1 | convolution fusion | flops 415236096 | bytes 4508672 | tf_op jit(solution)/shard_map/while/body/eval_jaxpr/dot_general | solution.py:14
  57.3 10.2 %fusion.25 = bf16[16,512,4096]{2,1,0:T(8,128)(2,1)} fusion(bf16[16,512,4096]{2,1,0:T(8,128)(2,1)} %get-tuple-element.121, s32[]{:T(128)} %get-tuple-element.120, f32[16,4096]{1,0:T(8,128)S(1)} %get-tuple-element.130, f32[4096]{0:T(1024)S(1)} %get-tuple-element.129, f32[512]{0:T(512)S(1)} %fusion.24, f32[16,16,512]{2,1,0:T(8,128)S(1)} %get-tuple-element.128), kind=kOutput, calls=%fused_computation.2.clone.1 | convolution fusion | flops 415236096 | bytes 4508672 | tf_op jit(solution)/shard_map/while/body/eval_jaxpr/dot_general | solution.py:14
  67.5 10.2 %fusion.25 = bf16[16,512,4096]{2,1,0:T(8,128)(2,1)} fusion(bf16[16,512,4096]{2,1,0:T(8,128)(2,1)} %get-tuple-element.121, s32[]{:T(128)} %get-tuple-element.120, f32[16,4096]{1,0:T(8,128)S(1)} %get-tuple-element.130, f32[4096]{0:T(1024)S(1)} %get-tuple-element.129, f32[512]{0:T(512)S(1)} %fusion.24, f32[16,16,512]{2,1,0:T(8,128)S(1)} %get-tuple-element.128), kind=kOutput, calls=%fused_computation.2.clone.1 | convolution fusion | flops 415236096 | bytes 4508672 | tf_op jit(solution)/shard_map/while/body/eval_jaxpr/dot_general | solution.py:14
  77.8 10.2 %fusion.25 = bf16[16,512,4096]{2,1,0:T(8,128)(2,1)} fusion(bf16[16,512,4096]{2,1,0:T(8,128)(2,1)} %get-tuple-element.121, s32[]{:T(128)} %get-tuple-element.120, f32[16,4096]{1,0:T(8,128)S(1)} %get-tuple-element.130, f32[4096]{0:T(1024)S(1)} %get-tuple-element.129, f32[512]{0:T(512)S(1)} %fusion.24, f32[16,16,512]{2,1,0:T(8,128)S(1)} %get-tuple-element.128), kind=kOutput, calls=%fused_computation.2.clone.1 | convolution fusion | flops 415236096 | bytes 4508672 | tf_op jit(solution)/shard_map/while/body/eval_jaxpr/dot_general | solution.py:14
  88.0 10.2 %fusion.25 = bf16[16,512,4096]{2,1,0:T(8,128)(2,1)} fusion(bf16[16,512,4096]{2,1,0:T(8,128)(2,1)} %get-tuple-element.121, s32[]{:T(128)} %get-tuple-element.120, f32[16,4096]{1,0:T(8,128)S(1)} %get-tuple-element.130, f32[4096]{0:T(1024)S(1)} %get-tuple-element.129, f32[512]{0:T(512)S(1)} %fusion.24, f32[16,16,512]{2,1,0:T(8,128)S(1)} %get-tuple-element.128), kind=kOutput, calls=%fused_computation.2.clone.1 | convolution fusion | flops 415236096 | bytes 4508672 | tf_op jit(solution)/shard_map/while/body/eval_jaxpr/dot_general | solution.py:14
  98.2 10.2 %fusion.25 = bf16[16,512,4096]{2,1,0:T(8,128)(2,1)} fusion(bf16[16,512,4096]{2,1,0:T(8,128)(2,1)} %get-tuple-element.121, s32[]{:T(128)} %get-tuple-element.120, f32[16,4096]{1,0:T(8,128)S(1)} %get-tuple-element.130, f32[4096]{0:T(1024)S(1)} %get-tuple-element.129, f32[512]{0:T(512)S(1)} %fusion.24, f32[16,16,512]{2,1,0:T(8,128)S(1)} %get-tuple-element.128), kind=kOutput, calls=%fused_computation.2.clone.1 | convolution fusion | flops 415236096 | bytes 4508672 | tf_op jit(solution)/shard_map/while/body/eval_jaxpr/dot_general | solution.py:14
  108.4 10.2 %fusion.25 = bf16[16,512,4096]{2,1,0:T(8,128)(2,1)} fusion(bf16[16,512,4096]{2,1,0:T(8,128)(2,1)} %get-tuple-element.121, s32[]{:T(128)} %get-tuple-element.120, f32[16,4096]{1,0:T(8,128)S(1)} %get-tuple-element.130, f32[4096]{0:T(1024)S(1)} %get-tuple-element.129, f32[512]{0:T(512)S(1)} %fusion.24, f32[16,16,512]{2,1,0:T(8,128)S(1)} %get-tuple-element.128), kind=kOutput, calls=%fused_computation.2.clone.1 | convolution fusion | flops 415236096 | bytes 4508672 | tf_op jit(solution)/shard_map/while/body/eval_jaxpr/dot_general | solution.py:14
  118.6 10.3 %fusion.25 = bf16[16,512,4096]{2,1,0:T(8,128)(2,1)} fusion(bf16[16,512,4096]{2,1,0:T(8,128)(2,1)} %get-tuple-element.121, s32[]{:T(128)} %get-tuple-element.120, f32[16,4096]{1,0:T(8,128)S(1)} %get-tuple-element.130, f32[4096]{0:T(1024)S(1)} %get-tuple-element.129, f32[512]{0:T(512)S(1)} %fusion.24, f32[16,16,512]{2,1,0:T(8,128)S(1)} %get-tuple-element.128), kind=kOutput, calls=%fused_computation.2.clone.1 | convolution fusion | flops 415236096 | bytes 4508672 | tf_op jit(solution)/shard_map/while/body/eval_jaxpr/dot_general | solution.py:14
  128.9 10.2 %fusion.25 = bf16[16,512,4096]{2,1,0:T(8,128)(2,1)} fusion(bf16[16,512,4096]{2,1,0:T(8,128)(2,1)} %get-tuple-element.121, s32[]{:T(128)} %get-tuple-element.120, f32[16,4096]{1,0:T(8,128)S(1)} %get-tuple-element.130, f32[4096]{0:T(1024)S(1)} %get-tuple-element.129, f32[512]{0:T(512)S(1)} %fusion.24, f32[16,16,512]{2,1,0:T(8,128)S(1)} %get-tuple-element.128), kind=kOutput, calls=%fused_computation.2.clone.1 | convolution fusion | flops 415236096 | bytes 4508672 | tf_op jit(solution)/shard_map/while/body/eval_jaxpr/dot_general | solution.py:14
  139.2 10.2 %fusion.25 = bf16[16,512,4096]{2,1,0:T(8,128)(2,1)} fusion(bf16[16,512,4096]{2,1,0:T(8,128)(2,1)} %get-tuple-element.121, s32[]{:T(128)} %get-tuple-element.120, f32[16,4096]{1,0:T(8,128)S(1)} %get-tuple-element.130, f32[4096]{0:T(1024)S(1)} %get-tuple-element.129, f32[512]{0:T(512)S(1)} %fusion.24, f32[16,16,512]{2,1,0:T(8,128)S(1)} %get-tuple-element.128), kind=kOutput, calls=%fused_computation.2.clone.1 | convolution fusion | flops 415236096 | bytes 4508672 | tf_op jit(solution)/shard_map/while/body/eval_jaxpr/dot_general | solution.py:14
  149.4 10.2 %fusion.25 = bf16[16,512,4096]{2,1,0:T(8,128)(2,1)} fusion(bf16[16,512,4096]{2,1,0:T(8,128)(2,1)} %get-tuple-element.121, s32[]{:T(128)} %get-tuple-element.120, f32[16,4096]{1,0:T(8,128)S(1)} %get-tuple-element.130, f32[4096]{0:T(1024)S(1)} %get-tuple-element.129, f32[512]{0:T(512)S(1)} %fusion.24, f32[16,16,512]{2,1,0:T(8,128)S(1)} %get-tuple-element.128), kind=kOutput, calls=%fused_computation.2.clone.1 | convolution fusion | flops 415236096 | bytes 4508672 | tf_op jit(solution)/shard_map/while/body/eval_jaxpr/dot_general | solution.py:14
  159.6 10.3 %fusion.25 = bf16[16,512,4096]{2,1,0:T(8,128)(2,1)} fusion(bf16[16,512,4096]{2,1,0:T(8,128)(2,1)} %get-tuple-element.121, s32[]{:T(128)} %get-tuple-element.120, f32[16,4096]{1,0:T(8,128)S(1)} %get-tuple-element.130, f32[4096]{0:T(1024)S(1)} %get-tuple-element.129, f32[512]{0:T(512)S(1)} %fusion.24, f32[16,16,512]{2,1,0:T(8,128)S(1)} %get-tuple-element.128), kind=kOutput, calls=%fused_computation.2.clone.1 | convolution fusion | flops 415236096 | bytes 4508672 | tf_op jit(solution)/shard_map/while/body/eval_jaxpr/dot_general | solution.py:14
  169.9 10.2 %fusion.25 = bf16[16,512,4096]{2,1,0:T(8,128)(2,1)} fusion(bf16[16,512,4096]{2,1,0:T(8,128)(2,1)} %get-tuple-element.121, s32[]{:T(128)} %get-tuple-element.120, f32[16,4096]{1,0:T(8,128)S(1)} %get-tuple-element.130, f32[4096]{0:T(1024)S(1)} %get-tuple-element.129, f32[512]{0:T(512)S(1)} %fusion.24, f32[16,16,512]{2,1,0:T(8,128)S(1)} %get-tuple-element.128), kind=kOutput, calls=%fused_computation.2.clone.1 | convolution fusion | flops 415236096 | bytes 4508672 | tf_op jit(solution)/shard_map/while/body/eval_jaxpr/dot_general | solution.py:14
  180.1 10.2 %fusion.25 = bf16[16,512,4096]{2,1,0:T(8,128)(2,1)} fusion(bf16[16,512,4096]{2,1,0:T(8,128)(2,1)} %get-tuple-element.121, s32[]{:T(128)} %get-tuple-element.120, f32[16,4096]{1,0:T(8,128)S(1)} %get-tuple-element.130, f32[4096]{0:T(1024)S(1)} %get-tuple-element.129, f32[512]{0:T(512)S(1)} %fusion.24, f32[16,16,512]{2,1,0:T(8,128)S(1)} %get-tuple-element.128), kind=kOutput, calls=%fused_computation.2.clone.1 | convolution fusion | flops 415236096 | bytes 4508672 | tf_op jit(solution)/shard_map/while/body/eval_jaxpr/dot_general | solution.py:14
  190.3 10.2 %fusion.25 = bf16[16,512,4096]{2,1,0:T(8,128)(2,1)} fusion(bf16[16,512,4096]{2,1,0:T(8,128)(2,1)} %get-tuple-element.121, s32[]{:T(128)} %get-tuple-element.120, f32[16,4096]{1,0:T(8,128)S(1)} %get-tuple-element.130, f32[4096]{0:T(1024)S(1)} %get-tuple-element.129, f32[512]{0:T(512)S(1)} %fusion.24, f32[16,16,512]{2,1,0:T(8,128)S(1)} %get-tuple-element.128), kind=kOutput, calls=%fused_computation.2.clone.1 | convolution fusion | flops 415236096 | bytes 4508672 | tf_op jit(solution)/shard_map/while/body/eval_jaxpr/dot_general | solution.py:14
  200.5 0.0 all-gather.4.cloned.1.call-done
  200.5 0.0 copy-start
  200.5 29.2 %convolution_convert_fusion.2 = bf16[4096,128]{1,0:T(8,128)(2,1)} fusion(bf16[8192,4096]{1,0:T(8,128)(2,1)} %bitcast.3, bf16[8192,128]{1,0:T(8,128)(2,1)} %all-gather.4.cloned.1.call-done), kind=kOutput, calls=%fused_computation.10 | convolution fusion | flops 8590458880 | bytes 70254592 | tf_op jit(solution)/shard_map/dot_general | solution.py:105
  229.7 0.0 reduce-scatter.4.cloned.1.call-update
  229.7 0.0 all-gather.6.cloned.1.call-start
  229.7 28.3 %reduce-scatter.4.cloned.1.call-done = bf16[1024,128]{1,0:T(8,128)(2,1)} async-done(((bf16[4096,128]{1,0:T(8,128)(2,1)}), bf16[1024,128]{1,0:T(8,128)(2,1)}) %reduce-scatter.4.cloned.1.call-update) | async-done | bytes 262160 | tf_op jit(solution)/shard_map/reduce_scatter | solution.py:104
  258.1 0.0 copy-done
  258.1 1.1 multiply_reduce_fusion.3
  259.2 13.2 %psum.63 = f32[128]{0:T(128)S(1)} all-reduce(f32[128]{0:T(128)S(1)} %get-tuple-element.63), channel_id=1, replica_groups=mesh['row'=4,'col'=8] {'col'}, use_global_device_ids=true, to_apply=%region_6.7 | all-reduce | flops 128 | bytes 1024 | tf_op jit(solution)/shard_map/psum | solution.py:116
  272.4 9.3 %psum.64 = f32[128]{0:T(128)S(1)} all-reduce(f32[128]{0:T(128)S(1)} %psum.63), channel_id=1, replica_groups=mesh['row'=4,'col'=8] {'row'}, use_global_device_ids=true, to_apply=%region_7.8 | all-reduce | flops 128 | bytes 1024 | tf_op jit(solution)/shard_map/psum | solution.py:116
  281.7 38.8 %psum.65 = f32[128]{0:T(128)S(1)} all-reduce(f32[128]{0:T(128)S(1)} %get-tuple-element.62), channel_id=1, replica_groups=mesh['row'=4,'col'=8] {'row','col'}, use_global_device_ids=true, to_apply=%region_9.10 | all-reduce | flops 128 | bytes 1024 | tf_op jit(solution)/shard_map/psum | solution.py:100
  320.5 0.0 copy-start.1
  320.6 1.9 fusion.10
  322.4 0.0 all-gather.6.cloned.1.call-update
  322.4 0.0 reduce-scatter.6.cloned.1.call-start
  322.5 26.9 %all-gather.6.cloned.1.call-done = bf16[8192,128]{1,0:T(8,128)(2,1)} async-done(((bf16[1024,128]{1,0:T(8,128)(2,1)}), bf16[8192,128]{1,0:T(8,128)(2,1)}) %all-gather.6.cloned.1.call-update) | async-done | bytes 2097168 | tf_op jit(solution)/shard_map/all_gather | solution.py:102
  349.4 29.1 %convolution_convert_fusion.1 = bf16[4096,128]{1,0:T(8,128)(2,1)} fusion(bf16[8192,4096]{1,0:T(8,128)(2,1)} %bitcast.3, bf16[8192,128]{1,0:T(8,128)(2,1)} %all-gather.6.cloned.1.call-done), kind=kOutput, calls=%fused_computation.9 | convolution fusion | flops 8590458880 | bytes 70254592 | tf_op jit(solution)/shard_map/dot_general | solution.py:105
  378.5 0.0 reduce-scatter.6.cloned.1.call-update
  378.5 0.0 all-gather.8.cloned.1.call-start
  378.6 27.4 %reduce-scatter.6.cloned.1.call-done = bf16[1024,128]{1,0:T(8,128)(2,1)} async-done(((bf16[4096,128]{1,0:T(8,128)(2,1)}), bf16[1024,128]{1,0:T(8,128)(2,1)}) %reduce-scatter.6.cloned.1.call-update) | async-done | bytes 262160 | tf_op jit(solution)/shard_map/reduce_scatter | solution.py:104
  406.0 1.1 multiply_reduce_fusion.2
  407.1 13.2 %psum.67 = f32[128]{0:T(128)S(1)} all-reduce(f32[128]{0:T(128)S(1)} %get-tuple-element.61), channel_id=1, replica_groups=mesh['row'=4,'col'=8] {'col'}, use_global_device_ids=true, to_apply=%region_14.15 | all-reduce | flops 128 | bytes 1024 | tf_op jit(solution)/shard_map/psum | solution.py:116
  420.3 9.2 %psum.68 = f32[128]{0:T(128)S(1)} all-reduce(f32[128]{0:T(128)S(1)} %psum.67), channel_id=1, replica_groups=mesh['row'=4,'col'=8] {'row'}, use_global_device_ids=true, to_apply=%region_15.16 | all-reduce | flops 128 | bytes 1024 | tf_op jit(solution)/shard_map/psum | solution.py:116
  429.4 38.8 %psum.66 = f32[128]{0:T(128)S(1)} all-reduce(f32[128]{0:T(128)S(1)} %get-tuple-element.60), channel_id=1, replica_groups=mesh['row'=4,'col'=8] {'row','col'}, use_global_device_ids=true, to_apply=%region_11.12 | all-reduce | flops 128 | bytes 1024 | tf_op jit(solution)/shard_map/psum | solution.py:100
  468.3 1.9 fusion.9
  470.2 0.0 all-gather.8.cloned.1.call-update
  470.2 0.3 reduce-scatter.8.cloned.1.call-start
  470.5 26.7 %all-gather.8.cloned.1.call-done = bf16[8192,128]{1,0:T(8,128)(2,1)} async-done(((bf16[1024,128]{1,0:T(8,128)(2,1)}), bf16[8192,128]{1,0:T(8,128)(2,1)}) %all-gather.8.cloned.1.call-update) | async-done | bytes 2097168 | tf_op jit(solution)/shard_map/all_gather | solution.py:102
  497.2 29.1 %convolution_convert_fusion = bf16[4096,128]{1,0:T(8,128)(2,1)} fusion(bf16[8192,4096]{1,0:T(8,128)(2,1)} %bitcast.3, bf16[8192,128]{1,0:T(8,128)(2,1)} %all-gather.8.cloned.1.call-done), kind=kOutput, calls=%fused_computation.8 | convolution fusion | flops 8590458880 | bytes 70254592 | tf_op jit(solution)/shard_map/dot_general | solution.py:105
  526.3 0.0 reduce-scatter.8.cloned.1.call-update
  526.3 27.4 %reduce-scatter.8.cloned.1.call-done = bf16[1024,128]{1,0:T(8,128)(2,1)} async-done(((bf16[4096,128]{1,0:T(8,128)(2,1)}), bf16[1024,128]{1,0:T(8,128)(2,1)}) %reduce-scatter.8.cloned.1.call-update) | async-done | bytes 262160 | tf_op jit(solution)/shard_map/reduce_scatter | solution.py:104
  553.8 1.1 multiply_reduce_fusion
  554.9 13.2 %psum.70 = f32[128]{0:T(128)S(1)} all-reduce(f32[128]{0:T(128)S(1)} %get-tuple-element.59), channel_id=1, replica_groups=mesh['row'=4,'col'=8] {'col'}, use_global_device_ids=true, to_apply=%region_20.21 | all-reduce | flops 128 | bytes 1024 | tf_op jit(solution)/shard_map/psum | solution.py:116
  568.1 9.2 %psum.71 = f32[128]{0:T(128)S(1)} all-reduce(f32[128]{0:T(128)S(1)} %psum.70), channel_id=1, replica_groups=mesh['row'=4,'col'=8] {'row'}, use_global_device_ids=true, to_apply=%region_21.22 | all-reduce | flops 128 | bytes 1024 | tf_op jit(solution)/shard_map/psum | solution.py:116
  577.2 38.8 %psum.69 = f32[128]{0:T(128)S(1)} all-reduce(f32[128]{0:T(128)S(1)} %get-tuple-element.58), channel_id=1, replica_groups=mesh['row'=4,'col'=8] {'row','col'}, use_global_device_ids=true, to_apply=%region_17.18 | all-reduce | flops 128 | bytes 1024 | tf_op jit(solution)/shard_map/psum | solution.py:100
  616.0 0.0 copy-done.1
  616.0 2.0 multiply_add_fusion.1
  (21 shorter events, 0.5 us)
Async XLA Ops:
  7.2 193.3 %all-gather.4.cloned.1.call-start = ((), (), s32[]{:S(2)}) async-start(), calls=%async_computation.3 | async-start | bytes 2359296 | tf_op jit(solution)/shard_map/all_gather | solution.py:102
  9.1 249.0 %reduce-scatter.4.cloned.1.call-start = ((), (), s32[]{:S(2)}) async-start(), calls=%async_computation.4 | async-start | bytes 1310720 | tf_op jit(solution)/shard_map/reduce_scatter | solution.py:104
  200.5 57.5 %copy-start = (s32[1024,128]{1,0:T(8,128)S(1)}, s32[1024,128]{1,0:T(8,128)}, u32[]{:S(2)}) copy-start(s32[1024,128]{1,0:T(8,128)} %param.7) | copy-start | bytes 1572868
  229.7 119.7 %all-gather.6.cloned.1.call-start = ((), (), s32[]{:S(2)}) async-start(), calls=%async_computation.5 | async-start | bytes 2359296 | tf_op jit(solution)/shard_map/all_gather | solution.py:102
  320.5 295.5 %copy-start.1 = (f32[128]{0:T(128)}, f32[128]{0:T(128)S(1)}, u32[]{:S(2)}) copy-start(f32[128]{0:T(128)S(1)} %get-tuple-element.81) | copy-start | bytes 1540
  322.4 83.5 %reduce-scatter.6.cloned.1.call-start = ((), (), s32[]{:S(2)}) async-start(), calls=%async_computation.6 | async-start | bytes 1310720 | tf_op jit(solution)/shard_map/reduce_scatter | solution.py:104
  378.5 118.6 %all-gather.8.cloned.1.call-start = ((), (), s32[]{:S(2)}) async-start(), calls=%async_computation.7 | async-start | bytes 2359296 | tf_op jit(solution)/shard_map/all_gather | solution.py:102
  470.2 83.6 %reduce-scatter.8.cloned.1.call-start = ((), (), s32[]{:S(2)}) async-start(), calls=%async_computation.8 | async-start | bytes 1310720 | tf_op jit(solution)/shard_map/reduce_scatter | solution.py:104
Sparse Core Ops, SparseCore 0:
  9.9 31.1 all-gather.3
  229.8 28.1 reduce-scatter.3
  322.6 26.7 all-gather.5
  378.7 27.2 reduce-scatter.5
  470.3 26.8 all-gather.7
  526.4 27.2 reduce-scatter.7
